TPU v7x, 32 devices: a whole 2x2x4 slice. The times are simulated.
32 devices in a mesh: row: 8 (over z, y), col: 4 (over x, core).
Axes of the slice: x: 2, y: 2, z: 4, core: 2. Of those that a mesh axis runs over, the one named last changes fastest.
Arguments:
- embeddings: bfloat16 [12288, 768], P(('row', 'col'))
- doc_order: int32 [12288], P(('row', 'col')), may hold values from 0 to 12287, each once
Outputs:
- nearest_earlier: float32 [12288], P(('row', 'col'))
Inputs may be any that keep to these rules, and one draw needn't show every extreme that they name: `doc_order`: each value 0 to 12287 appears once.
All inputs are finite; a program needn't handle non-finite values.
Results may differ from a plain program's by a relative error of at most 0.00051.
Values may be sent and summed in bfloat16 or wider, within the bound.
No kernel may reach another device: no remote copies, remote signals or barrier semaphores. Data moves between devices by JAX's collectives and lax.ppermute only.
A program may use at most 64 MiB of HBM per device.

v0:
```python
import jax
import jax.numpy as jnp
from jax import lax
from jax.sharding import PartitionSpec as P


def normalize_rows(embeddings):
    floats = embeddings.astype(jnp.float32)
    scale = lax.rsqrt(jnp.sum(floats * floats, axis=1, keepdims=True) + 1e-06)
    return (floats * scale).astype(jnp.bfloat16)


def block_size(length):
    width = min(512, length)
    while length % width != 0:
        width = width - 1
    return width


def masked_maxima(row_units, row_orders, col_units, col_orders, running):
    length = col_units.shape[0]
    width = block_size(length)
    col_groups = col_units.reshape(length // width, width, col_units.shape[1])
    order_groups = col_orders.reshape(length // width, width)

    def one_block(current, pair):
        units_here, orders_here = pair
        scores = jnp.dot(row_units, units_here.T, preferred_element_type=jnp.float32)
        earlier = orders_here[None, :] < row_orders[:, None]
        masked = jnp.where(earlier, scores, jnp.float32(-1.0))
        return (jnp.maximum(current, jnp.max(masked, axis=1)), None)

    result, unused = lax.scan(one_block, running, (col_groups, order_groups))
    return result


def shards(embeddings, doc_order):
    unit_rows = normalize_rows(embeddings)
    own_rows = unit_rows.shape[0]
    col_count = lax.axis_size("col")
    block_rows = own_rows * col_count
    initial = jnp.full((block_rows,), -1.0, jnp.float32)
    row_units, row_orders = (
        lax.all_gather(unit_rows, "col", axis=0, tiled=True),
        lax.all_gather(doc_order, "col", axis=0, tiled=True),
    )
    best_rows = masked_maxima(
        row_units,
        row_orders,
        lax.all_gather(unit_rows, "row", axis=0, tiled=True),
        lax.all_gather(doc_order, "row", axis=0, tiled=True),
        initial,
    )
    whole_max = lax.pmax(best_rows, "col")
    own_share = lax.dynamic_slice_in_dim(whole_max, lax.axis_index("col") * own_rows, own_rows, 0)
    return jnp.maximum(own_share, jnp.float32(-1.0))


def solution(mesh):
    return jax.shard_map(
        shards,
        mesh=mesh,
        in_specs=(P(("row", "col"), None), P(("row", "col"))),
        out_specs=P(("row", "col")),
        check_vma=False,
    )
```

profile of v0, /device:TPU:0, one launch (start us, length us, event | category | flops | bytes accessed | tf_op | source)
XLA Modules:
  0.0 152.0 jit_solution(297163370144080767)
XLA Ops:
  6.5 0.0 copy-start
  6.5 0.0 all-gather.7.cloned.1.call-start
  6.5 1.3 fusion.5
  7.8 2.0 %fusion.6 = bf16[384,768]{1,0:T(8,128)(2,1)} fusion(bf16[384,768]{1,0:T(8,128)(2,1)} %param.4, f32[384]{0:T(512)S(1)} %add_rsqrt_fusion), kind=kLoop, calls=%fused_computation.11 | loop fusion | flops 884736 | bytes 1181184 | tf_op jit(solution)/shard_map/convert_element_type | solution.py:10
  9.9 0.0 all-gather.7.cloned.1.call-update
  9.9 0.0 all-gather.5.cloned.1.call-start
  9.9 0.7 all-gather.5.cloned.1.call-update
  10.7 0.0 copy-done
  10.7 27.8 %all-gather = s32[8,1,384]{2,1,0:T(1,128)S(1)} all-gather(s32[1,1,384]{2,1,0:T(1,128)S(1)} %reshape.15), channel_id=1, replica_groups=mesh['row'=8,'col'=4] {'row'}, dimensions={0}, use_global_device_ids=true | all-gather | bytes 13824 | tf_op jit(solution)/shard_map/all_gather | solution.py:51
  38.6 5.2 %all-gather.1 = s32[4,1,384]{2,1,0:T(1,128)S(1)} all-gather(s32[1,1,384]{2,1,0:T(1,128)S(1)} %reshape.15), channel_id=1, replica_groups=mesh['row'=8,'col'=4] {'col'}, dimensions={0}, use_global_device_ids=true | all-gather | bytes 7680 | tf_op jit(solution)/shard_map/all_gather | solution.py:45
  43.8 0.0 all-gather.7.cloned.1.call-done
  43.8 74.5 %all-gather.5.cloned.1.call-done = bf16[3072,768]{1,0:T(8,128)(2,1)} async-done(((bf16[384,768]{1,0:T(8,128)(2,1)}), bf16[3072,768]{1,0:T(8,128)(2,1)}) %all-gather.5.cloned.1.call-update) | async-done | bytes 4718608 | tf_op jit(solution)/shard_map/all_gather | solution.py:50
  118.3 20.4 %while.11 = (s32[]{:T(128)}, f32[1536]{0:T(1024)S(1)}, s32[6,512]{1,0:T(8,128)S(1)}, s32[1536]{0:T(1024)S(1)}, bf16[6,512,768]{2,1,0:T(8,128)(2,1)}, /*index=5*/bf16[1536,768]{1,0:T(8,128)(2,1)}, s32[]{:T(128)}, s32[]{:T(128)}) while((s32[]{:T(128)}, f32[1536]{0:T(1024)S(1)}, s32[6,512]{1,0:T(8,128)S(1)}, s32[1536]{0:T(1024)S(1)}, ...), condition=%wide.region_3.4_spmd.clone, body=%wide.region_1.3_spmd.clone.sunk | while | flops 1210320384 | bytes 3183203 | solution.py:33
  118.4 3.3 %fusion.13 = f32[1536]{0:T(1024)S(1)} fusion(bf16[1536,768]{1,0:T(8,128)(2,1)} %get-tuple-element.129, s32[1536]{0:T(1024)S(1)} %get-tuple-element.127, s32[512]{0:T(512)S(1)} %bitcast.20, bf16[6,512,768]{2,1,0:T(8,128)(2,1)} %get-tuple-element.128, s32[]{:T(128)} %get-tuple-element.116), kind=kOutput, calls=%fused_computation.2.clone.1 | convolution fusion | flops 1210317312 | bytes 3160576 | tf_op jit(solution)/shard_map/while/body/eval_jaxpr/dot_general | solution.py:28
  121.8 3.3 %fusion.13 = f32[1536]{0:T(1024)S(1)} fusion(bf16[1536,768]{1,0:T(8,128)(2,1)} %get-tuple-element.129, s32[1536]{0:T(1024)S(1)} %get-tuple-element.127, s32[512]{0:T(512)S(1)} %bitcast.20, bf16[6,512,768]{2,1,0:T(8,128)(2,1)} %get-tuple-element.128, s32[]{:T(128)} %get-tuple-element.116), kind=kOutput, calls=%fused_computation.2.clone.1 | convolution fusion | flops 1210317312 | bytes 3160576 | tf_op jit(solution)/shard_map/while/body/eval_jaxpr/dot_general | solution.py:28
  125.2 3.3 %fusion.13 = f32[1536]{0:T(1024)S(1)} fusion(bf16[1536,768]{1,0:T(8,128)(2,1)} %get-tuple-element.129, s32[1536]{0:T(1024)S(1)} %get-tuple-element.127, s32[512]{0:T(512)S(1)} %bitcast.20, bf16[6,512,768]{2,1,0:T(8,128)(2,1)} %get-tuple-element.128, s32[]{:T(128)} %get-tuple-element.116), kind=kOutput, calls=%fused_computation.2.clone.1 | convolution fusion | flops 1210317312 | bytes 3160576 | tf_op jit(solution)/shard_map/while/body/eval_jaxpr/dot_general | solution.py:28
  128.6 3.3 %fusion.13 = f32[1536]{0:T(1024)S(1)} fusion(bf16[1536,768]{1,0:T(8,128)(2,1)} %get-tuple-element.129, s32[1536]{0:T(1024)S(1)} %get-tuple-element.127, s32[512]{0:T(512)S(1)} %bitcast.20, bf16[6,512,768]{2,1,0:T(8,128)(2,1)} %get-tuple-element.128, s32[]{:T(128)} %get-tuple-element.116), kind=kOutput, calls=%fused_computation.2.clone.1 | convolution fusion | flops 1210317312 | bytes 3160576 | tf_op jit(solution)/shard_map/while/body/eval_jaxpr/dot_general | solution.py:28
  132.0 3.3 %fusion.13 = f32[1536]{0:T(1024)S(1)} fusion(bf16[1536,768]{1,0:T(8,128)(2,1)} %get-tuple-element.129, s32[1536]{0:T(1024)S(1)} %get-tuple-element.127, s32[512]{0:T(512)S(1)} %bitcast.20, bf16[6,512,768]{2,1,0:T(8,128)(2,1)} %get-tuple-element.128, s32[]{:T(128)} %get-tuple-element.116), kind=kOutput, calls=%fused_computation.2.clone.1 | convolution fusion | flops 1210317312 | bytes 3160576 | tf_op jit(solution)/shard_map/while/body/eval_jaxpr/dot_general | solution.py:28
  135.4 3.3 %fusion.13 = f32[1536]{0:T(1024)S(1)} fusion(bf16[1536,768]{1,0:T(8,128)(2,1)} %get-tuple-element.129, s32[1536]{0:T(1024)S(1)} %get-tuple-element.127, s32[512]{0:T(512)S(1)} %bitcast.20, bf16[6,512,768]{2,1,0:T(8,128)(2,1)} %get-tuple-element.128, s32[]{:T(128)} %get-tuple-element.116), kind=kOutput, calls=%fused_computation.2.clone.1 | convolution fusion | flops 1210317312 | bytes 3160576 | tf_op jit(solution)/shard_map/while/body/eval_jaxpr/dot_general | solution.py:28
  138.7 5.8 %pmax.7 = f32[1536]{0:T(1024)S(1)} all-reduce(f32[1536]{0:T(1024)S(1)} %get-tuple-element.37), channel_id=1, replica_groups=mesh['row'=8,'col'=4] {'col'}, use_global_device_ids=true, to_apply=%region_4.5 | all-reduce | flops 1536 | bytes 12288 | tf_op jit(solution)/shard_map/pmax | solution.py:54
  144.5 0.7 dynamic-slice_maximum_fusion
  (19 shorter events, 0.2 us)
Async XLA Ops:
  6.5 4.1 %copy-start = (s32[384]{0:T(512)S(1)}, s32[384]{0:T(512)}, u32[]{:S(2)}) copy-start(s32[384]{0:T(512)} %param.5) | copy-start | bytes 4612
  6.5 37.3 %all-gather.7.cloned.1.call-start = ((), (), s32[]{:S(2)}) async-start(), calls=%async_computation.1 | async-start | bytes 2949120 | tf_op jit(solution)/shard_map/all_gather | solution.py:44
  9.9 108.5 %all-gather.5.cloned.1.call-start = ((), (), s32[]{:S(2)}) async-start(), calls=%async_computation | async-start | bytes 5308416 | tf_op jit(solution)/shard_map/all_gather | solution.py:50
Sparse Core Ops, SparseCore 0:
  10.0 26.7 all-gather.6
  39.0 79.3 all-gather.4
where the time goes:
time: 152 us
  waiting for transfers between devices  75.3 us (50%)
  blocking collectives  38.8 us (26%)
  matrix products  20.1 us (13%)
  between operations  13.5 us (9%)
  other arithmetic  4.08 us (3%)
    all_gather x1, waiting for transfers between devices, shards(): lax.all_gather(unit_rows, 'row', axis=0, tiled=True)  74.5 us
    all_gather x1, blocking collectives, shards(): lax.all_gather(doc_order, 'row', axis=0, tiled=True)  27.8 us
    dot_general x6, matrix products, one_block(): jnp.dot(row_units, units_here.T, preferred_element_type=jnp.float32)  20.1 us
    pmax x1, blocking collectives, shards(): whole_max = lax.pmax(best_rows, 'col')  5.77 us
    all_gather x1, blocking collectives, shards(): lax.all_gather(doc_order, 'col', axis=0, tiled=True)  5.18 us
  transfers between devices with their start and end apart: 2, of which 1 were waited for; matrix products, arithmetic and copies ran while one was open for 0% of the time, Pallas kernels for 0%

commit v1 on v0

--- a/solution.py
+++ b/solution.py
@@ -2,6 +2,18 @@
 import jax.numpy as jnp
 from jax import lax
 from jax.sharding import PartitionSpec as P
+
+
+def collect(array, axis, dim):
+    ways, here = (lax.axis_size(axis), lax.axis_index(axis))
+    grown, reach = (array, 1)
+    while reach < ways:
+        theirs = lax.ppermute(grown, axis, [(d, d ^ reach) for d in range(ways)])
+        mine_first = jnp.concatenate([grown, theirs], axis=dim)
+        theirs_first = jnp.concatenate([theirs, grown], axis=dim)
+        grown = jnp.where(here & reach == 0, mine_first, theirs_first)
+        reach = 2 * reach
+    return grown
 
 
 def normalize_rows(embeddings):
@@ -48,7 +60,7 @@
         row_units,
         row_orders,
         lax.all_gather(unit_rows, "row", axis=0, tiled=True),
-        lax.all_gather(doc_order, "row", axis=0, tiled=True),
+        collect(doc_order, "row", 0),
         initial,
     )
     whole_max = lax.pmax(best_rows, "col")

time: 152 us -> 152 us (level)
  blocking collectives: 38.8 us -> 11.1 us
  waiting for transfers between devices: 75.3 us -> 94.8 us
  starting transfers between devices: 0.04 us -> 8.28 us
    all_gather x1 -> x0, blocking collectives: 27.8 us -> none  [shards(): lax.all_gather(doc_order, 'row', axis=0, tiled=True)]
    all_gather x1, waiting for transfers between devices: 0.02 us -> 9.37 us  [shards(): lax.all_gather(unit_rows, 'col', axis=0, tiled=True)]
    ppermute x0 -> x3, starting transfers between devices: none -> 8.23 us  [collect(): theirs = lax.ppermute(grown, axis, [(d, d ^ reach) for d in range(ways)])]
    all_gather x1, waiting for transfers between devices: 74.5 us -> 81.5 us  [shards(): lax.all_gather(unit_rows, 'row', axis=0, tiled=True)]
    ppermute x0 -> x3, waiting for transfers between devices: none -> 3.15 us  [collect(): theirs = lax.ppermute(grown, axis, [(d, d ^ reach) for d in range(ways)])]
  transfers between devices with their start and end apart: 2 -> 5, of which waited for: 1 -> 4; matrix products, arithmetic and copies ran while one was open for 0% -> 0% of each run, Pallas kernels for 0% -> 0%
where the time goes in v1:
time: 152 us
  waiting for transfers between devices  94.8 us (62%)
  matrix products  20.1 us (13%)
  between operations  13.5 us (9%)
  blocking collectives  11.1 us (7%)
  starting transfers between devices  8.28 us (5%)
  other arithmetic  4.07 us (3%)
    all_gather x1, waiting for transfers between devices, shards(): lax.all_gather(unit_rows, 'row', axis=0, tiled=True)  81.5 us
    dot_general x6, matrix products, one_block(): jnp.dot(row_units, units_here.T, preferred_element_type=jnp.float32)  20.1 us
    all_gather x1, waiting for transfers between devices, shards(): lax.all_gather(unit_rows, 'col', axis=0, tiled=True)  9.37 us
    ppermute x3, starting transfers between devices, collect(): theirs = lax.ppermute(grown, axis, [(d, d ^ reach) for d in range(ways)])  8.23 us
    pmax x1, blocking collectives, shards(): whole_max = lax.pmax(best_rows, 'col')  5.77 us
    all_gather x1, blocking collectives, shards(): lax.all_gather(doc_order, 'col', axis=0, tiled=True)  5.32 us
    ppermute x3, waiting for transfers between devices, collect(): theirs = lax.ppermute(grown, axis, [(d, d ^ reach) for d in range(ways)])  3.15 us
  transfers between devices with their start and end apart: 5, of which 4 were waited for; matrix products, arithmetic and copies ran while one was open for 0% of the time, Pallas kernels for 0%

profile of v1, /device:TPU:0, one launch (start us, length us, event | category | flops | bytes accessed | tf_op | source)
XLA Modules:
  0.0 152.1 jit_solution(14440633916514864618)
XLA Ops:
  6.5 0.0 copy-start
  6.5 0.0 all-gather.6.cloned.1.call-start
  6.5 1.3 fusion.5
  7.8 2.0 %fusion.6 = bf16[384,768]{1,0:T(8,128)(2,1)} fusion(bf16[384,768]{1,0:T(8,128)(2,1)} %param.4, f32[384]{0:T(512)S(1)} %add_rsqrt_fusion), kind=kLoop, calls=%fused_computation.11 | loop fusion | flops 884736 | bytes 1181184 | tf_op jit(solution)/shard_map/convert_element_type | solution.py:22
  9.9 0.0 all-gather.6.cloned.1.call-update
  9.9 0.0 all-gather.4.cloned.1.call-start
  9.9 0.7 all-gather.4.cloned.1.call-update
  10.6 0.0 copy-done
  10.6 3.1 %collective-permute-start = (s32[384]{0:T(512)S(1)}, s32[384]{0:T(512)S(1)}, u32[]{:S(2)}, u32[]{:S(2)}) collective-permute-start(s32[384]{0:T(512)S(1)} %copy-done), channel_id=1, source_target_pairs={{0,4},{4,0},{8,12},{12,8},{16,20},{20,16},{24,28},{28,24},{1,5},{5... | collective-permute-start | bytes 4616 | tf_op jit(solution)/shard_map/ppermute | solution.py:11
  13.7 1.6 %collective-permute-done = s32[384]{0:T(512)S(1)} collective-permute-done((s32[384]{0:T(512)S(1)}, s32[384]{0:T(512)S(1)}, u32[]{:S(2)}, u32[]{:S(2)}) %collective-permute-start) | collective-permute-done | bytes 1568 | tf_op jit(solution)/shard_map/ppermute | solution.py:11
  15.3 2.1 %collective-permute-start.1 = (s32[768]{0:T(1024)S(1)}, s32[768]{0:T(1024)S(1)}, u32[]{:S(2)}, u32[]{:S(2)}) collective-permute-start(s32[768]{0:T(1024)S(1)} %add_select_fusion.2), channel_id=1, source_target_pairs={{0,8},{4,12},{8,0},{12,4},{16,24},{20,28},{24,16},{28,20},{1,9},{5... | collective-permute-start | bytes 9224 | tf_op jit(solution)/shard_map/ppermute | solution.py:11
  17.4 1.6 %collective-permute-done.1 = s32[768]{0:T(1024)S(1)} collective-permute-done((s32[768]{0:T(1024)S(1)}, s32[768]{0:T(1024)S(1)}, u32[]{:S(2)}, u32[]{:S(2)}) %collective-permute-start.1) | collective-permute-done | bytes 3104 | tf_op jit(solution)/shard_map/ppermute | solution.py:11
  18.9 3.1 %collective-permute-start.2 = (s32[1536]{0:T(1024)S(1)}, s32[1536]{0:T(1024)S(1)}, u32[]{:S(2)}, u32[]{:S(2)}) collective-permute-start(s32[1536]{0:T(1024)S(1)} %add_select_fusion.1), channel_id=1, source_target_pairs={{0,16},{4,20},{8,24},{12,28},{16,0},{20,4},{24,8},{28,12},{1,17},{... | collective-permute-start | bytes 18440 | tf_op jit(solution)/shard_map/ppermute | solution.py:11
  22.0 5.3 %all-gather = s32[4,1,384]{2,1,0:T(1,128)S(1)} all-gather(s32[1,1,384]{2,1,0:T(1,128)S(1)} %reshape.20), channel_id=1, replica_groups=mesh['row'=8,'col'=4] {'col'}, dimensions={0}, use_global_device_ids=true | all-gather | bytes 7680 | tf_op jit(solution)/shard_map/all_gather | solution.py:57
  27.4 0.0 collective-permute-done.2
  27.5 9.4 %all-gather.6.cloned.1.call-done = bf16[1536,768]{1,0:T(8,128)(2,1)} async-done(((bf16[384,768]{1,0:T(8,128)(2,1)}), bf16[1536,768]{1,0:T(8,128)(2,1)}) %all-gather.6.cloned.1.call-update) | async-done | bytes 2359312 | tf_op jit(solution)/shard_map/all_gather | solution.py:56
  36.8 81.5 %all-gather.4.cloned.1.call-done = bf16[3072,768]{1,0:T(8,128)(2,1)} async-done(((bf16[384,768]{1,0:T(8,128)(2,1)}), bf16[3072,768]{1,0:T(8,128)(2,1)}) %all-gather.4.cloned.1.call-update) | async-done | bytes 4718608 | tf_op jit(solution)/shard_map/all_gather | solution.py:62
  118.4 20.4 %while.11 = (s32[]{:T(128)}, f32[1536]{0:T(1024)S(1)}, s32[6,512]{1,0:T(8,128)S(1)}, s32[1536]{0:T(1024)S(1)}, bf16[6,512,768]{2,1,0:T(8,128)(2,1)}, /*index=5*/bf16[1536,768]{1,0:T(8,128)(2,1)}, s32[]{:T(128)}, s32[]{:T(128)}) while((s32[]{:T(128)}, f32[1536]{0:T(1024)S(1)}, s32[6,512]{1,0:T(8,128)S(1)}, s32[1536]{0:T(1024)S(1)}, ...), condition=%wide.region_3.4_spmd.clone, body=%wide.region_1.3_spmd.clone.sunk | while | flops 1210320384 | bytes 3183203 | solution.py:45
  118.4 3.3 %fusion.13 = f32[1536]{0:T(1024)S(1)} fusion(bf16[1536,768]{1,0:T(8,128)(2,1)} %get-tuple-element.129, s32[1536]{0:T(1024)S(1)} %get-tuple-element.127, s32[512]{0:T(512)S(1)} %bitcast.20, bf16[6,512,768]{2,1,0:T(8,128)(2,1)} %get-tuple-element.128, s32[]{:T(128)} %get-tuple-element.116), kind=kOutput, calls=%fused_computation.2.clone.1 | convolution fusion | flops 1210317312 | bytes 3160576 | tf_op jit(solution)/shard_map/while/body/eval_jaxpr/dot_general | solution.py:40
  121.8 3.3 %fusion.13 = f32[1536]{0:T(1024)S(1)} fusion(bf16[1536,768]{1,0:T(8,128)(2,1)} %get-tuple-element.129, s32[1536]{0:T(1024)S(1)} %get-tuple-element.127, s32[512]{0:T(512)S(1)} %bitcast.20, bf16[6,512,768]{2,1,0:T(8,128)(2,1)} %get-tuple-element.128, s32[]{:T(128)} %get-tuple-element.116), kind=kOutput, calls=%fused_computation.2.clone.1 | convolution fusion | flops 1210317312 | bytes 3160576 | tf_op jit(solution)/shard_map/while/body/eval_jaxpr/dot_general | solution.py:40
  125.2 3.3 %fusion.13 = f32[1536]{0:T(1024)S(1)} fusion(bf16[1536,768]{1,0:T(8,128)(2,1)} %get-tuple-element.129, s32[1536]{0:T(1024)S(1)} %get-tuple-element.127, s32[512]{0:T(512)S(1)} %bitcast.20, bf16[6,512,768]{2,1,0:T(8,128)(2,1)} %get-tuple-element.128, s32[]{:T(128)} %get-tuple-element.116), kind=kOutput, calls=%fused_computation.2.clone.1 | convolution fusion | flops 1210317312 | bytes 3160576 | tf_op jit(solution)/shard_map/while/body/eval_jaxpr/dot_general | solution.py:40
  128.6 3.3 %fusion.13 = f32[1536]{0:T(1024)S(1)} fusion(bf16[1536,768]{1,0:T(8,128)(2,1)} %get-tuple-element.129, s32[1536]{0:T(1024)S(1)} %get-tuple-element.127, s32[512]{0:T(512)S(1)} %bitcast.20, bf16[6,512,768]{2,1,0:T(8,128)(2,1)} %get-tuple-element.128, s32[]{:T(128)} %get-tuple-element.116), kind=kOutput, calls=%fused_computation.2.clone.1 | convolution fusion | flops 1210317312 | bytes 3160576 | tf_op jit(solution)/shard_map/while/body/eval_jaxpr/dot_general | solution.py:40
  132.0 3.3 %fusion.13 = f32[1536]{0:T(1024)S(1)} fusion(bf16[1536,768]{1,0:T(8,128)(2,1)} %get-tuple-element.129, s32[1536]{0:T(1024)S(1)} %get-tuple-element.127, s32[512]{0:T(512)S(1)} %bitcast.20, bf16[6,512,768]{2,1,0:T(8,128)(2,1)} %get-tuple-element.128, s32[]{:T(128)} %get-tuple-element.116), kind=kOutput, calls=%fused_computation.2.clone.1 | convolution fusion | flops 1210317312 | bytes 3160576 | tf_op jit(solution)/shard_map/while/body/eval_jaxpr/dot_general | solution.py:40
  135.4 3.3 %fusion.13 = f32[1536]{0:T(1024)S(1)} fusion(bf16[1536,768]{1,0:T(8,128)(2,1)} %get-tuple-element.129, s32[1536]{0:T(1024)S(1)} %get-tuple-element.127, s32[512]{0:T(512)S(1)} %bitcast.20, bf16[6,512,768]{2,1,0:T(8,128)(2,1)} %get-tuple-element.128, s32[]{:T(128)} %get-tuple-element.116), kind=kOutput, calls=%fused_computation.2.clone.1 | convolution fusion | flops 1210317312 | bytes 3160576 | tf_op jit(solution)/shard_map/while/body/eval_jaxpr/dot_general | solution.py:40
  138.8 5.8 %pmax.7 = f32[1536]{0:T(1024)S(1)} all-reduce(f32[1536]{0:T(1024)S(1)} %get-tuple-element.37), channel_id=1, replica_groups=mesh['row'=8,'col'=4] {'col'}, use_global_device_ids=true, to_apply=%region_4.5 | all-reduce | flops 1536 | bytes 12288 | tf_op jit(solution)/shard_map/pmax | solution.py:66
  144.6 0.7 dynamic-slice_maximum_fusion
  (22 shorter events, 0.2 us)
Async XLA Ops:
  6.5 4.1 %copy-start = (s32[384]{0:T(512)S(1)}, s32[384]{0:T(512)}, u32[]{:S(2)}) copy-start(s32[384]{0:T(512)} %param.5) | copy-start | bytes 4612
  6.5 30.3 %all-gather.6.cloned.1.call-start = ((), (), s32[]{:S(2)}) async-start(), calls=%async_computation.1 | async-start | bytes 2949120 | tf_op jit(solution)/shard_map/all_gather | solution.py:56
  9.9 108.5 %all-gather.4.cloned.1.call-start = ((), (), s32[]{:S(2)}) async-start(), calls=%async_computation | async-start | bytes 5308416 | tf_op jit(solution)/shard_map/all_gather | solution.py:62
  10.6 4.6 %collective-permute-start = (s32[384]{0:T(512)S(1)}, s32[384]{0:T(512)S(1)}, u32[]{:S(2)}, u32[]{:S(2)}) collective-permute-start(s32[384]{0:T(512)S(1)} %copy-done), channel_id=1, source_target_pairs={{0,4},{4,0},{8,12},{12,8},{16,20},{20,16},{24,28},{28,24},{1,5},{5... | collective-permute-start | bytes 4616 | tf_op jit(solution)/shard_map/ppermute | solution.py:11
  15.3 3.7 %collective-permute-start.1 = (s32[768]{0:T(1024)S(1)}, s32[768]{0:T(1024)S(1)}, u32[]{:S(2)}, u32[]{:S(2)}) collective-permute-start(s32[768]{0:T(1024)S(1)} %add_select_fusion.2), channel_id=1, source_target_pairs={{0,8},{4,12},{8,0},{12,4},{16,24},{20,28},{24,16},{28,20},{1,9},{5... | collective-permute-start | bytes 9224 | tf_op jit(solution)/shard_map/ppermute | solution.py:11
  18.9 8.5 %collective-permute-start.2 = (s32[1536]{0:T(1024)S(1)}, s32[1536]{0:T(1024)S(1)}, u32[]{:S(2)}, u32[]{:S(2)}) collective-permute-start(s32[1536]{0:T(1024)S(1)} %add_select_fusion.1), channel_id=1, source_target_pairs={{0,16},{4,20},{8,24},{12,28},{16,0},{20,4},{24,8},{28,12},{1,17},{... | collective-permute-start | bytes 18440 | tf_op jit(solution)/shard_map/ppermute | solution.py:11
Sparse Core Ops, SparseCore 0:
  10.0 26.7 all-gather.5
  39.0 79.3 all-gather.3
